TPU v7x, 128 devices: a whole 4x4x4 slice. The times are simulated.
128 devices in a mesh: section: 2 (over core), tp: 8 (over z_lo, x), fsdp: 8 (over z_hi, y).
Axes of the slice: x: 4, y: 4, z: 4 (z_hi: 2, z_lo: 2; z = z_hi * 2 + z_lo), core: 2. Of those that a mesh axis runs over, the one named last changes fastest.
Arguments:
- normed: bfloat16 [2, 1024, 4608], P('section', 'tp', 'fsdp'), may hold values from -6 to 6
- cotangent: bfloat16 [2, 1024, 4608], P('section', 'tp', 'fsdp'), may hold values from -6 to 6
- w_gate: bfloat16 [2, 4608, 18432], P('section', 'fsdp', 'tp'), may hold values from -0.09375 to 0.09375
- w_up: bfloat16 [2, 4608, 18432], P('section', 'fsdp', 'tp'), may hold values from -0.09375 to 0.09375
- w_down: bfloat16 [2, 4608, 18432], P('section', 'fsdp', 'tp'), may hold values from -0.046875 to 0.046875
Outputs:
- passed: bfloat16 [2, 1024, 4608], P('section', 'tp', 'fsdp')
- grad_gate: bfloat16 [2, 4608, 18432], P('section', 'fsdp', 'tp')
- grad_up: bfloat16 [2, 4608, 18432], P('section', 'fsdp', 'tp')
- grad_down: bfloat16 [2, 4608, 18432], P('section', 'fsdp', 'tp')
All inputs are finite; a program needn't handle non-finite values.
Results may differ from a plain program's by a relative error of at most 0.012.
Values may be sent and summed in bfloat16 or wider, within the bound.
A program may use at most 192 MiB of HBM per device.

v0:
```python
import math

import jax
import jax.numpy as jnp
from jax import lax
from jax.sharding import PartitionSpec as P


def from_everyone(x, axis):
    copies = jnp.broadcast_to(x, (lax.axis_size(axis), *x.shape))
    return lax.all_to_all(copies, axis, split_axis=0, concat_axis=0, tiled=True)


def laid_out(parts, dim):
    parts = jnp.moveaxis(parts, 0, dim)
    lengths = parts.shape
    return parts.reshape(*lengths[:dim], lengths[dim] * lengths[dim + 1], *lengths[dim + 2 :])


def gathered_copies(x, axis, dim):
    parts = from_everyone(x, axis)
    return laid_out(parts, dim)


def sent_together(arrays, axis, dim, along):
    ends, at = ([], 0)
    for a in arrays[:-1]:
        at += a.shape[along]
        ends.append(at)
    both = jnp.concatenate(arrays, axis=along)
    return tuple(jnp.split(gathered_copies(both, axis, dim), ends, axis=along))


def in_one_piece(arrays, axis, dim, along):
    ends, at = ([], 0)
    for a in arrays[:-1]:
        at += a.shape[along]
        ends.append(at)
    both = jnp.concatenate(arrays, axis=along)
    return tuple(jnp.split(lax.all_gather(both, axis, axis=dim, tiled=True), ends, axis=along))


def in_blocks(x, dim, length):
    lengths = x.shape
    parts = x.reshape(*lengths[:dim], length, lengths[dim] // length, *lengths[dim + 1 :])
    return jnp.moveaxis(parts, dim, 0)


def summed_on_arrival(x, axis, dim):
    parts = in_blocks(x, dim, lax.axis_size(axis))
    arrived = lax.all_to_all(parts, axis, split_axis=0, concat_axis=0, tiled=True)
    return arrived.astype(jnp.float32).sum(axis=0)


def from_behind(value, axis, steps):
    count = lax.axis_size(axis)
    pairs = [(source, (source + steps) % count) for source in range(count)]
    return lax.ppermute(value, axis, pairs)


def activate(gate, up, back):
    coeff = math.sqrt(2.0 / math.pi)
    inner = jnp.tanh(coeff * (gate + 0.044715 * gate * gate * gate))
    act = 0.5 * gate * (1.0 + inner)
    slope = 0.5 * (1.0 + inner) + 0.5 * gate * (1.0 - inner * inner) * coeff * (
        1.0 + 3.0 * 0.044715 * gate * gate
    )
    hidden = (act * up).astype(jnp.bfloat16)
    d_gate = (back * up * slope).astype(jnp.bfloat16)
    d_up = (back * act).astype(jnp.bfloat16)
    return (hidden, d_gate, d_up)


def column_grad(left, right):
    return lax.dot_general(
        left, right, (((0,), (0,)), ((), ())), preferred_element_type=jnp.float32
    )


def row_back(grads, weight):
    return lax.dot_general(
        grads, weight, (((1,), (1,)), ((), ())), preferred_element_type=jnp.float32
    )


def local(normed, cotangent, w_gate, w_up, w_down):
    rows_own = normed[0]
    cot_own = cotangent[0]
    wgate = w_gate[0]
    wup = w_up[0]
    wdown = w_down[0]
    rows_all, cot_all = sent_together((rows_own, cot_own), "tp", 0, 1)
    total = rows_all.shape[0]
    width = wgate.shape[1]
    scale = 1.0 / math.sqrt(total)
    gate = jnp.dot(rows_all, wgate, preferred_element_type=jnp.float32)
    up = jnp.dot(rows_all, wup, preferred_element_type=jnp.float32)
    back = jnp.dot(cot_all, wdown, preferred_element_type=jnp.float32)
    summed = lax.psum_scatter(
        jnp.concatenate((gate, up, back), axis=1), "fsdp", scatter_dimension=0, tiled=True
    )
    part_hidden, part_gate, part_up = activate(
        summed[:, :width], summed[:, width : 2 * width], summed[:, 2 * width :]
    )
    hidden, d_gate, d_up = in_one_piece((part_hidden, part_gate, part_up), "fsdp", 0, 1)
    grad_gate = (column_grad(rows_all, d_gate) * scale).astype(jnp.bfloat16)
    grad_up = (column_grad(rows_all, d_up) * scale).astype(jnp.bfloat16)
    grad_down = (column_grad(cot_all, hidden) * scale).astype(jnp.bfloat16)
    branch = summed_on_arrival(
        (row_back(d_gate, wgate) + row_back(d_up, wup)).astype(jnp.bfloat16), "tp", 0
    )
    handed = (cot_own.astype(jnp.float32) + branch).astype(jnp.bfloat16)
    passed = from_behind(handed, "section", 1)
    return (passed[None], grad_gate[None], grad_up[None], grad_down[None])


def solution(mesh):
    in_specs = (
        P("section", "tp", "fsdp"),
        P("section", "tp", "fsdp"),
        P("section", "fsdp", "tp"),
        P("section", "fsdp", "tp"),
        P("section", "fsdp", "tp"),
    )
    out_specs = (
        P("section", "tp", "fsdp"),
        P("section", "fsdp", "tp"),
        P("section", "fsdp", "tp"),
        P("section", "fsdp", "tp"),
    )
    return jax.shard_map(local, mesh=mesh, in_specs=in_specs, out_specs=out_specs, check_vma=False)
```

profile of v0, /device:TPU:0, one launch (start us, length us, event | category | flops | bytes accessed | tf_op | source)
XLA Modules:
  0.0 589.5 jit_solution(10289725890272365546)
XLA Ops:
  7.2 0.0 copy-start
  7.2 0.0 reduce-scatter.2.cloned.1.call-start
  7.2 1.2 pad_maximum_fusion.2
  8.4 0.2 copy.10
  8.6 0.3 broadcast_in_dim.15
  8.9 35.3 %all_to_all.10 = bf16[8,128,1152]{2,1,0:T(8,128)(2,1)S(1)} all-to-all(bf16[8,128,1152]{2,1,0:T(8,128)(2,1)S(1)} %broadcast_in_dim.15), channel_id=1, replica_groups=mesh['section'=2,'tp'=8,'fsdp'=8] {'tp'}, dimensions={0} | all-to-all | bytes 4718592 | tf_op jit(solution)/shard_map/all_to_all | solution.py:11
  44.2 0.0 copy-start.1
  44.2 0.0 copy-done
  44.2 0.0 copy-start.4
  44.2 6.2 %fusion.15 = f32[1024,2304]{1,0:T(8,128)} fusion(bf16[1,576,2304]{2,1,0:T(8,128)(2,1)S(1)} %copy-done, bf16[1024,1152]{1,0:T(8,128)(2,1)S(1)} %bitcast.34), kind=kOutput, calls=%fused_computation.17 | convolution fusion | flops 2717908992 | bytes 13402112 | tf_op jit(solution)/shard_map/dot_general | solution.py:97
  50.5 0.0 copy-done.4
  50.5 0.0 copy-start.5
  50.5 6.4 %fusion.12 = f32[1024,2304]{1,0:T(8,128)} fusion(bf16[1,576,2304]{2,1,0:T(8,128)(2,1)S(1)} %copy-done.4, bf16[1024,1152]{1,0:T(8,128)(2,1)S(1)} %bitcast.35), kind=kOutput, calls=%fused_computation.14 | convolution fusion | flops 2717908992 | bytes 13402112 | tf_op jit(solution)/shard_map/dot_general | solution.py:98
  56.8 0.0 copy-done.1
  56.8 0.0 copy-done.5
  56.8 6.1 %fusion.18 = f32[1024,2304]{1,0:T(8,128)} fusion(bf16[1,576,2304]{2,1,0:T(8,128)(2,1)S(1)} %copy-done.5, bf16[1024,1152]{1,0:T(8,128)(2,1)S(1)} %bitcast.36), kind=kOutput, calls=%fused_computation.20 | convolution fusion | flops 2717908992 | bytes 13402112 | tf_op jit(solution)/shard_map/dot_general | solution.py:96
  62.9 20.3 %pad_maximum_fusion = f32[1024,6912]{1,0:T(8,128)} fusion(f32[1024,2304]{1,0:T(8,128)} %fusion.12, f32[1024,2304]{1,0:T(8,128)} %fusion.15, f32[1024,2304]{1,0:T(8,128)} %fusion.18), kind=kLoop, calls=%fused_computation | loop fusion | flops 14155776 | bytes 56623104 | tf_op jit(solution)/shard_map/concatenate | solution.py:100
  83.2 0.0 reduce-scatter.2.cloned.1.call-update
  83.2 0.0 all-gather.2.cloned.1.call-start
  83.3 292.9 %reduce-scatter.2.cloned.1.call-done = f32[128,6912]{1,0:T(8,128)} async-done(((f32[1024,6912]{1,0:T(8,128)}), f32[128,6912]{1,0:T(8,128)}) %reduce-scatter.2.cloned.1.call-update) | async-done | bytes 3538960 | tf_op jit(solution)/shard_map/reduce_scatter | solution.py:99
  376.2 2.9 multiply_convert_fusion.4
  379.1 1.3 pad_maximum_fusion.1
  380.4 0.0 all-gather.2.cloned.1.call-update
  380.5 160.1 %all-gather.2.cloned.1.call-done = bf16[1024,6912]{1,0:T(8,128)(2,1)} async-done(((bf16[128,6912]{1,0:T(8,128)(2,1)}), bf16[1024,6912]{1,0:T(8,128)(2,1)}) %all-gather.2.cloned.1.call-update) | async-done | bytes 14155792 | tf_op jit(solution)/shard_map/all_gather | solution.py:40
  540.6 0.0 copy-start.6
  540.6 5.0 fusion.7
  545.5 0.0 copy-done.6
  545.5 5.3 fusion.24
  550.8 1.2 copy.14
  552.1 4.4 all-to-all-start.1
  556.5 0.0 copy-start.2
  556.5 7.3 %fusion.1 = bf16[1,576,2304]{2,1,0:T(8,128)(2,1)} fusion(bf16[1024,6912]{1,0:T(8,128)(2,1)} %all-gather.2.cloned.1.call-done, bf16[1024,1152]{1,0:T(8,128)(2,1)} %bitcast.37), kind=kOutput, calls=%fused_computation.5 | convolution fusion | flops 2720563200 | bytes 8683520 | tf_op jit(solution)/shard_map/dot_general | solution.py:75
  563.9 0.0 copy-done.2
  563.9 0.0 copy-start.3
  563.9 6.9 %fusion.2 = bf16[1,576,2304]{2,1,0:T(8,128)(2,1)} fusion(bf16[1024,6912]{1,0:T(8,128)(2,1)} %all-gather.2.cloned.1.call-done, bf16[1024,1152]{1,0:T(8,128)(2,1)S(1)} %bitcast.39), kind=kOutput, calls=%fused_computation.6 | convolution fusion | flops 2720563200 | bytes 8683520 | tf_op jit(solution)/shard_map/dot_general | solution.py:75
  570.7 2.3 all-to-all-done.1
  573.0 1.5 convert_reduce_fusion
  574.5 0.0 copy-done.3
  574.5 0.1 collective-permute-start
  574.6 7.4 %fusion.3 = bf16[1,576,2304]{2,1,0:T(8,128)(2,1)} fusion(bf16[1024,6912]{1,0:T(8,128)(2,1)} %all-gather.2.cloned.1.call-done, bf16[1024,1152]{1,0:T(8,128)(2,1)} %bitcast.38), kind=kOutput, calls=%fused_computation.7 | convolution fusion | flops 2720563200 | bytes 8683520 | tf_op jit(solution)/shard_map/dot_general | solution.py:75
  582.0 0.0 collective-permute-done
  582.0 0.7 copy.16
  (1 shorter events, 0.0 us)
Async XLA Ops:
  7.2 37.0 %copy-start = (bf16[1,576,2304]{2,1,0:T(8,128)(2,1)S(1)}, bf16[1,576,2304]{2,1,0:T(8,128)(2,1)}, u32[]{:S(2)}) copy-start(bf16[1,576,2304]{2,1,0:T(8,128)(2,1)} %param.8) | copy-start | bytes 7962628
  7.2 369.0 %reduce-scatter.2.cloned.1.call-start = ((), (), s32[]{:S(2)}) async-start(), calls=%async_computation.3 | async-start | bytes 31850496 | tf_op jit(solution)/shard_map/reduce_scatter | solution.py:99
  44.2 12.6 %copy-start.1 = (bf16[8,128,1152]{2,1,0:T(8,128)(2,1)}, bf16[8,128,1152]{2,1,0:T(8,128)(2,1)S(1)}, u32[]{:S(2)}) copy-start(bf16[8,128,1152]{2,1,0:T(8,128)(2,1)S(1)} %all_to_all.10) | copy-start | bytes 7077892
  44.2 6.2 %copy-start.4 = (bf16[1,576,2304]{2,1,0:T(8,128)(2,1)S(1)}, bf16[1,576,2304]{2,1,0:T(8,128)(2,1)}, u32[]{:S(2)}) copy-start(bf16[1,576,2304]{2,1,0:T(8,128)(2,1)} %param.9) | copy-start | bytes 7962628
  50.5 6.4 %copy-start.5 = (bf16[1,576,2304]{2,1,0:T(8,128)(2,1)S(1)}, bf16[1,576,2304]{2,1,0:T(8,128)(2,1)}, u32[]{:S(2)}) copy-start(bf16[1,576,2304]{2,1,0:T(8,128)(2,1)} %param.7) | copy-start | bytes 7962628
  83.2 457.3 %all-gather.2.cloned.1.call-start = ((), (), s32[]{:S(2)}) async-start(), calls=%async_computation.4 | async-start | bytes 15925248 | tf_op jit(solution)/shard_map/all_gather | solution.py:40
  540.6 5.0 copy-start.6
  552.1 20.9 %all-to-all-start.1 = ((bf16[8,128,576]{1,2,0:T(8,128)(2,1)}), bf16[8,128,576]{1,2,0:T(8,128)(2,1)}, u32[]{:S(2)}, u32[]{:S(2)}) async-start(bf16[8,128,576]{1,2,0:T(8,128)(2,1)} %bitcast.33), calls=%async_computation.2 | async-start | bytes 2359296 | tf_op jit(solution)/shard_map/all_to_all | solution.py:51
  556.5 7.4 %copy-start.2 = (bf16[8,128,1152]{2,1,0:T(8,128)(2,1)S(1)}, bf16[8,128,1152]{2,1,0:T(8,128)(2,1)}, u32[]{:S(2)}) copy-start(bf16[8,128,1152]{2,1,0:T(8,128)(2,1)} %copy-done.1) | copy-start | bytes 7077892
  563.9 10.6 %copy-start.3 = (bf16[1,128,576]{1,2,0:T(8,128)(2,1)S(1)}, bf16[1,128,576]{1,2,0:T(8,128)(2,1)}, u32[]{:S(2)}) copy-start(bf16[1,128,576]{1,2,0:T(8,128)(2,1)} %param.6) | copy-start | bytes 442372
  574.5 7.5 %collective-permute-start = (bf16[128,576]{0,1:T(8,128)(2,1)S(1)}, bf16[128,576]{0,1:T(8,128)(2,1)S(1)}, u32[]{:S(2)}, u32[]{:S(2)}) collective-permute-start(bf16[128,576]{0,1:T(8,128)(2,1)S(1)} %add_convert_fusion.1), channel_id=1, source_target_pairs={{0,64},{64,0},{1,65},{65,1},{2,66},{66,2},{3,67},{67,3},{4,68},{68... | collective-permute-start | bytes 442376 | tf_op jit(solution)/shard_map/ppermute | solution.py:58
Sparse Core Ops, SparseCore 0:
  83.3 292.8 reduce-scatter.1
  380.6 159.9 all-gather.1
where the time goes:
time: 591 us; the launch traced here: 590 us
  waiting for transfers between devices  455 us (77%)
  matrix products  50.6 us (9%)
  blocking collectives  35.3 us (6%)
  other arithmetic  27.1 us (5%)
  between operations  14.1 us (2%)
    reduce_scatter x1, waiting for transfers between devices, local(): lax.psum_scatter(jnp.concatenate((gate, up, back), axis=1), 'fsdp', scatt...  293 us
    all_gather x1, waiting for transfers between devices, in_one_piece(): lax.all_gather(both, axis, axis=dim, tiled=True)  160 us
    all_to_all x1, blocking collectives, from_everyone(): return lax.all_to_all(copies, axis, split_axis=0, concat_axis=0, tiled=True)  35.3 us
    dot_general x3, matrix products, column_grad(): lax.dot_general(left, right, (((0,), (0,)), ((), ())), preferred_element_...  21.6 us
    concatenate x1, other arithmetic, local(): jnp.concatenate((gate, up, back), axis=1)  20.3 us
  transfers between devices with their start and end apart: 4, of which 3 were waited for; matrix products, arithmetic and copies ran while one was open for 4% of the time, Pallas kernels for 0%

commit v1 on v0

v1 whole, which is shorter than its diff:
```python
import functools
import math

import jax
import jax.numpy as jnp
from jax import lax
from jax.experimental import pallas as pl
from jax.experimental.pallas import tpu as pltpu
from jax.sharding import PartitionSpec as P

MESH = pl.DeviceIdType.MESH
CHUNK = 256
LAGS = {"B": 1, "C": 2, "D": 3, "E": 4, "H": 5}
F32 = jnp.float32
BF16 = jnp.bfloat16


def activate(gate, up, back):
    coeff = math.sqrt(2.0 / math.pi)
    inner = jnp.tanh(coeff * (gate + 0.044715 * gate * gate * gate))
    act = 0.5 * gate * (1.0 + inner)
    slope = 0.5 * (1.0 + inner) + 0.5 * gate * (1.0 - inner * inner) * coeff * (
        1.0 + 3.0 * 0.044715 * gate * gate
    )
    return act * up, back * up * slope, back * act


def kernel(
    n_hbm, c_hbm, wg_hbm, wu_hbm, wd_hbm,
    passed, gg_hbm, gu_hbm, gd_hbm,
    rows, rows_t, weights, part, arrived, grads, branch, staged, leaving, landed, other_cot,
    load_sem, weight_sem, out_sem, head_sem, head_send, recv_sem, rs_send, ag_send, tail_recv, tail_send,
    cot_sem, cot_send,
):
    chunks = weights.shape[0]
    chunk = weights.shape[2] // 3
    total = 4 * 2 * rows.shape[3]
    half = rows.shape[3] // 2
    section = lax.axis_index("section")
    tp = lax.axis_index("tp")
    fsdp = lax.axis_index("fsdp")
    zl, x = tp // 4, tp % 4
    zh, y = fsdp // 4, fsdp % 4
    oz = 1 - zh
    ol = 1 - zl
    y1, y2, y3 = (y + 1) % 4, (y + 2) % 4, (y + 3) % 4
    x1, x2, x3 = (x + 1) % 4, (x + 2) % 4, (x + 3) % 4
    to_y1, to_y2, to_y3 = ({"fsdp": zh * 4 + k} for k in (y1, y2, y3))
    to_z = {"fsdp": oz * 4 + y}
    to_x1, to_x2, to_x3 = ({"tp": zl * 4 + k} for k in (x1, x2, x3))
    to_l = {"tp": ol * 4 + x}
    others = [{"section": 1 - section, "tp": t} for t in range(8)]

    for t in range(chunks):
        for k, hbm in enumerate((wg_hbm, wu_hbm, wd_hbm)):
            pltpu.make_async_copy(
                hbm.at[0, :, t * chunk : (t + 1) * chunk],
                weights.at[t, :, k * chunk : (k + 1) * chunk],
                weight_sem.at[t],
            ).start()
    own_n = pltpu.make_async_copy(n_hbm.at[0], rows.at[0, x, zl], load_sem.at[0])
    own_c = pltpu.make_async_copy(c_hbm.at[0], rows.at[1, x, zl], load_sem.at[1])
    own_n.start()
    own_c.start()

    barrier = pltpu.get_barrier_semaphore()
    peers = [to_y1, to_y2, to_y3, to_z, to_x1, to_x2, to_x3, to_l] + others
    for peer in peers:
        pl.semaphore_signal(barrier, inc=1, device_id=peer, device_id_type=MESH)
    pl.semaphore_wait(barrier, len(peers))

    def send(src, dst, send_sem, recv, peer):
        pltpu.make_async_remote_copy(
            src_ref=src, dst_ref=dst, send_sem=send_sem, recv_sem=recv, device_id=peer, device_id_type=MESH
        ).start()

    def wait_for(ref, sem):
        pltpu.make_async_copy(ref, ref, sem).wait()

    def head(k, xx, ll, to, sem):
        send(rows.at[k, xx, ll], rows.at[k, xx, ll], head_send.at[k], head_sem.at[sem], to)

    own_n.wait()
    head(0, x, zl, to_l, 1)
    for to in (to_x1, to_x3, to_x2):
        head(0, x, zl, to, 0)
    own_c.wait()
    for to in (to_x1, to_x3, to_x2):
        head(1, x, zl, to, 2)
    head(1, x, zl, to_l, 3)
    send(rows.at[1, x, zl], other_cot, cot_send, cot_sem, {"section": 1 - section})
    wait_for(rows.at[0, 0, 0], head_sem.at[1])
    for to in (to_x1, to_x3, to_x2):
        head(0, x, ol, to, 0)
    wait_for(rows.at[1, 0:3, 0], head_sem.at[2])
    for xx in (x1, x3, x2):
        head(1, xx, zl, to_l, 3)
    wait_for(rows.at[0, 0:3], head_sem.at[0])
    wait_for(rows.at[1, 0:2], head_sem.at[3])

    branch[...] = jnp.zeros_like(branch)

    def forward(c):
        wait_for(weights.at[c], weight_sem.at[c])

        def tile(k, _):
            n_tile = rows[0, k].reshape(4 * half, rows.shape[4])
            c_tile = rows[1, k].reshape(4 * half, rows.shape[4])
            gate_up = jnp.dot(n_tile, weights[c, :, : 2 * chunk], preferred_element_type=F32)
            part[c, k, :, :, : 2 * chunk] = gate_up.astype(BF16).reshape(2, 2 * half, 2 * chunk)
            back = jnp.dot(c_tile, weights[c, :, 2 * chunk :], preferred_element_type=F32)
            part[c, k, :, :, 2 * chunk :] = back.astype(BF16).reshape(2, 2 * half, chunk)
            return 0

        lax.fori_loop(0, 4, tile, 0)

    def add(dst, src):
        dst[...] = (dst[...].astype(F32) + src[...].astype(F32)).astype(BF16)

    def rs(src, dst, c, k, to):
        send(src, dst, rs_send.at[c], recv_sem.at[c, k], to)

    def ag(c, yy, zz, k, to):
        send(grads.at[c, yy, zz], grads.at[c, yy, zz], ag_send.at[c], recv_sem.at[c, k], to)

    def start_y(c):
        rs(part.at[c, y2, 0], arrived.at[c, 0], c, 0, to_y1)
        rs(part.at[c, y2, 1], arrived.at[c, 1], c, 0, to_y3)

    def start_z(c):
        for yy in (y2, y1, y3, y):
            rs(part.at[c, yy, oz], arrived.at[c, yy], c, 0, to_z)

    def second_y(c):
        wait_for(arrived.at[c, 0:2], recv_sem.at[c, 0])
        add(part.at[c, y1, 0], arrived.at[c, 0])
        rs(part.at[c, y1], arrived.at[c, 2:4], c, 1, to_y1)
        add(part.at[c, y3, 1], arrived.at[c, 1])
        rs(part.at[c, y3], arrived.at[c, 4:6], c, 1, to_y3)

    def second_z(c):
        wait_for(arrived.at[c, 0:4], recv_sem.at[c, 0])
        add(part.at[c, y2, zh], arrived.at[c, y2])
        rs(part.at[c, y2, zh, :half], arrived.at[c, 4, :half], c, 1, to_y1)
        rs(part.at[c, y2, zh, half:], arrived.at[c, 4, half:], c, 1, to_y3)
        add(part.at[c, y1, zh], arrived.at[c, y1])
        add(part.at[c, y3, zh], arrived.at[c, y3])

    def third_y(c):
        wait_for(arrived.at[c, 2:6], recv_sem.at[c, 1])
        part[c, y, oz] = (
            part[c, y, oz].astype(F32) + arrived[c, 2 + oz].astype(F32) + arrived[c, 4 + oz].astype(F32)
        ).astype(BF16)
        rs(part.at[c, y, oz], arrived.at[c, 6], c, 2, to_z)

    def third_z(c):
        wait_for(arrived.at[c, 4], recv_sem.at[c, 1])
        add(part.at[c, y1, zh, :half], arrived.at[c, 4, :half])
        rs(part.at[c, y1, zh], arrived.at[c, 5], c, 2, to_y1)
        add(part.at[c, y3, zh, half:], arrived.at[c, 4, half:])
        rs(part.at[c, y3, zh], arrived.at[c, 6], c, 2, to_y3)

    def finish(c, terms):
        summed = part[c, y, zh].astype(F32)
        for t in terms:
            summed = summed + arrived[c, t].astype(F32)
        hidden, d_gate, d_up = activate(summed[:, :chunk], summed[:, chunk : 2 * chunk], summed[:, 2 * chunk :])
        grads[c, y, zh, :, :chunk] = d_gate.astype(BF16)
        grads[c, y, zh, :, chunk : 2 * chunk] = d_up.astype(BF16)
        grads[c, y, zh, :, 2 * chunk :] = hidden.astype(BF16)

    def finish_y(c):
        wait_for(arrived.at[c, 6], recv_sem.at[c, 2])
        finish(c, (2 + zh, 4 + zh, 6))
        ag(c, y, zh, 3, to_z)
        for to in (to_y1, to_y3, to_y2):
            ag(c, y, zh, 4, to)

    def finish_z(c):
        wait_for(arrived.at[c, 5:7], recv_sem.at[c, 2])
        finish(c, (y, 5, 6))
        for to in (to_y1, to_y3, to_y2):
            ag(c, y, zh, 3, to)
        ag(c, y, zh, 4, to_z)

    def spread_y(c):
        wait_for(grads.at[c, 0, 0], recv_sem.at[c, 3])
        for to in (to_y1, to_y3, to_y2):
            ag(c, y, oz, 4, to)

    def spread_z(c):
        wait_for(grads.at[c, 0:3, 0], recv_sem.at[c, 3])
        for yy in (y1, y3, y2):
            ag(c, yy, zh, 4, to_z)

    def take_y(c):
        wait_for(grads.at[c, 0:3], recv_sem.at[c, 4])

    def take_z(c):
        wait_for(grads.at[c, 0:2], recv_sem.at[c, 4])

    def to_branch(c):
        def tile(k, _):
            g_tile = grads[c, k, :, :, : 2 * chunk].reshape(4 * half, 2 * chunk)
            back = lax.dot_general(
                g_tile, weights[c, :, : 2 * chunk], (((1,), (1,)), ((), ())), preferred_element_type=F32
            )
            branch[k] += back.reshape(2, 2 * half, back.shape[1])
            return 0

        lax.fori_loop(0, 4, tile, 0)

    def transposes():
        for k in range(2):
            for r in range(8):
                rows_t[k, :, r * 2 * half : (r + 1) * 2 * half] = rows[k, r // 2, r % 2].T

    outs = (gg_hbm, gu_hbm, gd_hbm)

    def weight_grads(c):
        slot = lax.rem(c, 2)

        @pl.when(c >= 2)
        def _():
            wait_for(staged.at[slot], out_sem.at[slot])

        m = rows_t.shape[1] // 3
        scale = 1.0 / math.sqrt(total)

        def tile(k, _):
            at = pl.ds(pl.multiple_of(k * m, m), m)
            d_in = grads[c, :, :, :, : 2 * chunk].reshape(total, 2 * chunk)
            a = jnp.dot(rows_t[0, at, :], d_in, preferred_element_type=F32) * scale
            staged[slot, at, : 2 * chunk] = a.astype(BF16)
            hid = grads[c, :, :, :, 2 * chunk :].reshape(total, chunk)
            b = jnp.dot(rows_t[1, at, :], hid, preferred_element_type=F32) * scale
            staged[slot, at, 2 * chunk :] = b.astype(BF16)
            return 0

        lax.fori_loop(0, 3, tile, 0)
        at = pl.ds(pl.multiple_of(c * chunk, chunk), chunk)
        for k, hbm in enumerate(outs):
            pltpu.make_async_copy(
                staged.at[slot, :, k * chunk : (k + 1) * chunk], hbm.at[0, :, at], out_sem.at[slot]
            ).start()

    def both(c, for_y, for_z):
        @pl.when((c >= 0) & (c < chunks) & (lax.rem(c, 2) == 0))
        def _():
            for_y(c)

        @pl.when((c >= 0) & (c < chunks) & (lax.rem(c, 2) == 1))
        def _():
            for_z(c)

    def step(i, _):
        @pl.when(i < chunks)
        def _():
            forward(i)

        both(i, start_y, start_z)
        both(i - LAGS["B"], second_y, second_z)
        both(i - LAGS["C"], third_y, third_z)
        both(i - LAGS["D"], finish_y, finish_z)
        both(i - LAGS["E"], spread_y, spread_z)

        @pl.when(i == 2)
        def _():
            transposes()

        c = i - LAGS["H"]
        both(c, take_y, take_z)

        @pl.when(c >= 0)
        def _():
            to_branch(c)

        @pl.when(c == chunks - 1)
        def _():
            for r in range(8):
                leaving[r] = branch[r // 2, r % 2].astype(BF16)
            for r in range(8):
                t = (r % 2) * 4 + r // 2
                send(leaving.at[r], landed.at[tp], tail_send, tail_recv, others[t])

        @pl.when(c >= 0)
        def _():
            weight_grads(c)

        return 0

    lax.fori_loop(0, chunks + LAGS["H"], step, 0)

    wait_for(other_cot, cot_sem)
    wait_for(landed, tail_recv)
    summed = landed[0].astype(F32)
    for r in range(1, 8):
        summed = summed + landed[r].astype(F32)
    passed[0] = (other_cot[...].astype(F32) + summed).astype(BF16)

    def drain(c, _):
        wait_for(arrived.at[c], rs_send.at[c])
        wait_for(arrived.at[c], ag_send.at[c])
        return 0

    lax.fori_loop(0, chunks, drain, 0)
    for k in range(2):
        wait_for(landed.at[0:7], head_send.at[k])
    wait_for(other_cot, cot_send)
    wait_for(leaving, tail_send)
    for slot in range(2):
        wait_for(staged.at[slot], out_sem.at[slot])


def local(normed, cotangent, w_gate, w_up, w_down):
    _, length, depth = normed.shape
    width = w_gate.shape[2]
    chunks = width // CHUNK
    wide = 3 * CHUNK
    anywhere = pl.BlockSpec(memory_space=pl.ANY)
    dma = pltpu.SemaphoreType.DMA
    return pl.pallas_call(
        kernel,
        out_shape=(
            jax.ShapeDtypeStruct(normed.shape, BF16),
            jax.ShapeDtypeStruct(w_gate.shape, BF16),
            jax.ShapeDtypeStruct(w_gate.shape, BF16),
            jax.ShapeDtypeStruct(w_gate.shape, BF16),
        ),
        in_specs=[anywhere] * 5,
        out_specs=(pl.BlockSpec(memory_space=pltpu.VMEM), anywhere, anywhere, anywhere),
        scratch_shapes=[
            pltpu.VMEM((2, 4, 2, length, depth), BF16),
            pltpu.VMEM((2, depth, 8 * length), BF16),
            pltpu.VMEM((chunks, depth, wide), BF16),
            pltpu.VMEM((chunks, 4, 2, length, wide), BF16),
            pltpu.VMEM((chunks, 7, length, wide), BF16),
            pltpu.VMEM((chunks, 4, 2, length, wide), BF16),
            pltpu.VMEM((4, 2, length, depth), F32),
            pltpu.VMEM((2, depth, wide), BF16),
            pltpu.VMEM((8, length, depth), BF16),
            pltpu.VMEM((8, length, depth), BF16),
            pltpu.VMEM((length, depth), BF16),
            dma((2,)),
            dma((chunks,)),
            dma((2,)),
            dma((4,)),
            dma((2,)),
            dma((chunks, 5)),
            dma((chunks,)),
            dma((chunks,)),
            dma(()),
            dma(()),
            dma(()),
            dma(()),
        ],
        compiler_params=pltpu.CompilerParams(
            collective_id=0, has_side_effects=True, vmem_limit_bytes=67_043_328
        ),
        name="geglu_relay",
    )(normed, cotangent, w_gate, w_up, w_down)


def solution(mesh):
    in_specs = (
        P("section", "tp", "fsdp"),
        P("section", "tp", "fsdp"),
        P("section", "fsdp", "tp"),
        P("section", "fsdp", "tp"),
        P("section", "fsdp", "tp"),
    )
    out_specs = (
        P("section", "tp", "fsdp"),
        P("section", "fsdp", "tp"),
        P("section", "fsdp", "tp"),
        P("section", "fsdp", "tp"),
    )
    return jax.shard_map(local, mesh=mesh, in_specs=in_specs, out_specs=out_specs, check_vma=False)
```

time: 591 us -> 281 us (0.48)
  waiting for transfers between devices: 455 us -> 0 us
  Pallas kernels: 0 us -> 265 us
  matrix products: 50.6 us -> 0 us
  blocking collectives: 35.3 us -> 0 us
  other arithmetic: 27.1 us -> 0 us
  between operations: 14.1 us -> 0.64 us
  local copies, waits for them, and re-layouts: 2.43 us -> 12.9 us
    reduce_scatter x1 -> x0, waiting for transfers between devices: 293 us -> none  [local(): lax.psum_scatter(jnp.concatenate((gate, up, back), axis=1), 'fsdp', scatt...]
    pallas_call x0 -> x1, Pallas kernels: none -> 265 us  [local(): pl.pallas_call(kernel, out_shape=(jax.ShapeDtypeStruct(normed.shape, BF16...]
    all_gather x1 -> x0, waiting for transfers between devices: 160 us -> none  [in_one_piece(): lax.all_gather(both, axis, axis=dim, tiled=True)]
    dot_general x8 -> x0, matrix products: 50.6 us -> none  [the longest x3 21.6 us: column_grad(): lax.dot_general(left, right, (((0,), (0,)), ((), ())), preferred_element_...]
    all_to_all x1 -> x0, blocking collectives: 35.3 us -> none  [from_everyone(): return lax.all_to_all(copies, axis, split_axis=0, concat_axis=0, tiled=True)]
    concatenate x3 -> x0, other arithmetic: 22.7 us -> none  [the longest x1 20.3 us: local(): jnp.concatenate((gate, up, back), axis=1)]
    unnamed x15 -> x9, local copies, waits for them, and re-layouts: 0.69 us -> 11.2 us
  transfers between devices with their start and end apart: 4 -> 0, of which waited for: 3 -> 0; matrix products, arithmetic and copies ran while one was open for 4% -> 0% of each run, Pallas kernels for 0% -> 0%
where the time goes in v1:
time: 281 us; the launch traced here: 279 us
  Pallas kernels  265 us (94%)
  local copies, waits for them, and re-layouts  12.9 us (5%)
    pallas_call x1, Pallas kernels, local(): pl.pallas_call(kernel, out_shape=(jax.ShapeDtypeStruct(normed.shape, BF16...  265 us
    unnamed x9, local copies, waits for them, and re-layouts  11.2 us

profile of v1, /device:TPU:0, one launch (start us, length us, event | category | flops | bytes accessed | tf_op | source)
XLA Modules:
  0.0 278.6 jit_solution(8111950735254673550)
XLA Ops:
  0.6 1.7 copy.9.n_hbm
  2.3 1.7 copy.10.c_hbm
  4.1 265.0 %geglu_relay.1 = (bf16[1,128,576]{2,1,0:T(8,128)(2,1)}, bf16[1,576,2304]{2,1,0:T(8,128)(2,1)}, bf16[1,576,2304]{2,1,0:T(8,128)(2,1)}, bf16[1,576,2304]{2,1,0:T(8,128)(2,1)}) custom-call(bf16[1,128,576]{2,1,0:T(8,128)(2,1)} %copy.9.n_hbm, bf16[1,128,576]{2,1,0:T(8,128)(2,1)} %copy.10.c_hbm, bf16[1,576,2304]{2,1,0:T(8,128)(2,1)} %wg_hbm.1, ...), custom_call_target="tpu_custom_call" | custom-call | tf_op jit(solution)/shard_map/geglu_relay/pallas_call | solution.py:322
  269.1 1.7 copy.11
  270.8 0.0 copy-start.1
  270.8 3.6 %copy.15 = bf16[1,576,2304]{2,1,0:T(8,128)(2,1)} copy(bf16[1,576,2304]{2,1,0:T(8,128)(2,1)} %get-tuple-element.13) | data formatting | bytes 5308416
  274.4 0.0 copy-done.1
  274.4 0.0 copy-start
  274.4 1.5 copy.16
  275.9 1.2 copy-done
  277.1 1.5 copy.17
Async XLA Ops:
  270.8 3.6 %copy-start.1 = (bf16[1,576,2304]{2,1,0:T(8,128)(2,1)S(1)}, bf16[1,576,2304]{2,1,0:T(8,128)(2,1)}, u32[]{:S(2)}) copy-start(bf16[1,576,2304]{2,1,0:T(8,128)(2,1)} %get-tuple-element.14) | copy-start | bytes 7962628
  274.4 2.7 copy-start

commit v2 on v0

v2 whole, which is shorter than its diff:
```python
import functools
import math

import jax
import jax.numpy as jnp
from jax import lax
from jax.experimental import pallas as pl
from jax.experimental.pallas import tpu as pltpu
from jax.sharding import PartitionSpec as P

MESH = pl.DeviceIdType.MESH
CHUNK = 256
LAG_SUM = ({"y": (0, 2, 3), "z": (0, 2, 3)}, {"y": (3, 4, 6), "z": (3, 4, 6)})
LAG_OUT = ({"y": (7, 8, 9, 10), "z": (7, 8, 9, 10)}, {"y": (13, 14, 15, 16), "z": (13, 14, 15, 17)})
LAST = 17
F32 = jnp.float32
BF16 = jnp.bfloat16


def activate(gate, up, back):
    coeff = math.sqrt(2.0 / math.pi)
    inner = jnp.tanh(coeff * (gate + 0.044715 * gate * gate * gate))
    act = 0.5 * gate * (1.0 + inner)
    slope = 0.5 * (1.0 + inner) + 0.5 * gate * (1.0 - inner * inner) * coeff * (
        1.0 + 3.0 * 0.044715 * gate * gate
    )
    return act * up, back * up * slope, back * act


def sums_z(c):
    return (c > 0) & (lax.rem(c, 2) == 0)


def spreads_z(c):
    return lax.rem(c, 2) == 1


def kernel(
    n_hbm, c_hbm, wg_hbm, wu_hbm, wd_hbm,
    passed, gg_hbm, gu_hbm, gd_hbm,
    own, rows, rows_t, weights, part0, part1, arrived0, arrived1, grads0, grads1, branch,
    staged0, staged1, leaving, landed, other_cot,
    load_sem, weight_sem, out_sem, head_sem, head_send, recv_sem, send_sem, tail_recv, tail_send, cot_sem, cot_send,
):
    parts, arriveds, gradss, stageds = (part0, part1), (arrived0, arrived1), (grads0, grads1), (staged0, staged1)
    chunks = weights.shape[0]
    chunk = weights.shape[2] // 3
    depth = rows.shape[4]
    length = rows.shape[3]
    half = length // 2
    total = 8 * length
    low, high = pl.ds(0, half), pl.ds(half, half)
    columns = (pl.ds(0, 2 * chunk), pl.ds(2 * chunk, chunk))
    section = lax.axis_index("section")
    tp = lax.axis_index("tp")
    fsdp = lax.axis_index("fsdp")
    zl, x = tp // 4, tp % 4
    zh, y = fsdp // 4, fsdp % 4
    oz = 1 - zh
    ol = 1 - zl
    y1, y2, y3 = (y + 1) % 4, (y + 2) % 4, (y + 3) % 4
    x1, x2, x3 = (x + 1) % 4, (x + 2) % 4, (x + 3) % 4
    to_y1, to_y3 = ({"fsdp": zh * 4 + k} for k in (y1, y3))
    to_z = {"fsdp": oz * 4 + y}
    to_x1, to_x2, to_x3 = ({"tp": zl * 4 + k} for k in (x1, x2, x3))
    to_l = {"tp": ol * 4 + x}
    others = [{"section": 1 - section, "tp": t} for t in range(8)]

    loads = [pltpu.make_async_copy(hbm.at[0], own.at[k], load_sem.at[k]) for k, hbm in enumerate((n_hbm, c_hbm))]
    for load in loads:
        load.start()

    barrier = pltpu.get_barrier_semaphore()
    peers = [to_y1, to_y3, to_z, to_x1, to_x2, to_x3, to_l] + others
    for peer in peers:
        pl.semaphore_signal(barrier, inc=1, device_id=peer, device_id_type=MESH)

    for t in range(chunks):
        for k, hbm in enumerate((wg_hbm, wu_hbm, wd_hbm)):
            pltpu.make_async_copy(
                hbm.at[0, :, t * chunk : (t + 1) * chunk],
                weights.at[t, :, k * chunk : (k + 1) * chunk],
                weight_sem.at[t, k // 2],
            ).start()

    for k, load in enumerate(loads):
        load.wait()
        rows[k, x, zl] = own[k].T

    def send(src, dst, sender, recv, peer):
        pltpu.make_async_remote_copy(
            src_ref=src, dst_ref=dst, send_sem=sender, recv_sem=recv, device_id=peer, device_id_type=MESH
        ).start()

    def wait_for(ref, sem):
        pltpu.make_async_copy(ref, ref, sem).wait()

    def head(k, xx, ll, which, sem, *peers):
        ref = rows.at[k, xx, ll, which]
        for peer in peers:
            send(ref, ref, head_send.at[k], head_sem.at[k, sem], peer)

    def head_start(k):
        head(k, x, zl, high, 2, to_x1, to_x3, to_x2)
        head(k, x, zl, low, 0, to_l)
        head(k, x, zl, high, 3, to_l)
        head(k, x, zl, low, 1, to_x1, to_x3, to_x2)

    def head_middle(k):
        wait_for(rows.at[k, 0, 0, low], head_sem.at[k, 0])
        head(k, x, ol, low, 1, to_x1, to_x3, to_x2)
        wait_for(rows.at[k, 0:3, 0, low], head_sem.at[k, 2])
        for xx in (x1, x3, x2):
            head(k, xx, zl, high, 3, to_l)

    def head_end(k):
        wait_for(rows.at[k, 0:3, 0], head_sem.at[k, 1])
        wait_for(rows.at[k, 0:2, 0], head_sem.at[k, 3])

    pl.semaphore_wait(barrier, len(peers))
    head_start(0)
    head_start(1)
    send(rows.at[1, x, zl], other_cot, cot_send, cot_sem, {"section": 1 - section})
    branch[...] = jnp.zeros_like(branch)
    head_middle(0)
    head_end(0)

    def forward(s, c):
        wait_for(weights.at[c, :, columns[s]], weight_sem.at[c, s])

        def tile(k, _):
            left = rows[s, k].reshape(2 * length, depth)
            out = jnp.dot(left, weights[c, :, columns[s]], preferred_element_type=F32)
            parts[s][c, k] = out.astype(BF16).reshape(2, length, out.shape[1])
            return 0

        lax.fori_loop(0, 4, tile, 0)

    def add(dst, src):
        dst[...] = (dst[...].astype(F32) + src[...].astype(F32)).astype(BF16)

    def move(src, dst, s, c, k, *peers):
        for peer in peers:
            send(src, dst, send_sem.at[k // 3, s, c], recv_sem.at[s, c, k], peer)

    def sum_y(s, stage, c):
        part, arrived = parts[s].at[c], arriveds[s].at[c]
        if stage == 0:
            forward(s, c)
            move(part.at[y2, 0], arrived.at[0], s, c, 0, to_y1)
            move(part.at[y2, 1], arrived.at[1], s, c, 0, to_y3)
        elif stage == 1:
            wait_for(arrived.at[0:2], recv_sem.at[s, c, 0])
            add(part.at[y1, 0], arrived.at[0])
            move(part.at[y1], arrived.at[2:4], s, c, 1, to_y1)
            add(part.at[y3, 1], arrived.at[1])
            move(part.at[y3], arrived.at[4:6], s, c, 1, to_y3)
        else:
            wait_for(arrived.at[2:6], recv_sem.at[s, c, 1])
            part[y, oz] = (
                part[y, oz].astype(F32) + arrived[2 + oz].astype(F32) + arrived[4 + oz].astype(F32)
            ).astype(BF16)
            move(part.at[y, oz], arrived.at[6], s, c, 2, to_z)

    def sum_z(s, stage, c):
        part, arrived = parts[s].at[c], arriveds[s].at[c]
        if stage == 0:
            forward(s, c)
            for yy in (y2, y1, y3, y):
                move(part.at[yy, oz], arrived.at[yy], s, c, 0, to_z)
        elif stage == 1:
            wait_for(arrived.at[0:4], recv_sem.at[s, c, 0])
            add(part.at[y2, zh], arrived.at[y2])
            move(part.at[y2, zh, low], arrived.at[4, low], s, c, 1, to_y1)
            move(part.at[y2, zh, high], arrived.at[4, high], s, c, 1, to_y3)
            add(part.at[y1, zh], arrived.at[y1])
            add(part.at[y3, zh], arrived.at[y3])
        else:
            wait_for(arrived.at[4], recv_sem.at[s, c, 1])
            add(part.at[y1, zh, low], arrived.at[4, low])
            move(part.at[y1, zh], arrived.at[5], s, c, 2, to_y1)
            add(part.at[y3, zh, high], arrived.at[4, high])
            move(part.at[y3, zh], arrived.at[6], s, c, 2, to_y3)

    def final_y(s, c):
        wait_for(arriveds[s].at[c, 6], recv_sem.at[s, c, 2])
        return final(s, c, (2 + zh, 4 + zh, 6))

    def final_z(s, c):
        wait_for(arriveds[s].at[c, 5:7], recv_sem.at[s, c, 2])
        return final(s, c, (y, 5, 6))

    def final(s, c, terms):
        out = parts[s][c, y, zh].astype(F32)
        for t in terms:
            out = out + arriveds[s][c, t].astype(F32)
        return out

    def finish(c, done):
        gate_up, back = done(0, c), done(1, c)
        hidden, d_gate, d_up = activate(gate_up[:, :chunk], gate_up[:, chunk:], back)
        grads0[c, y, zh, :, :chunk] = d_gate.astype(BF16)
        grads0[c, y, zh, :, chunk:] = d_up.astype(BF16)
        grads1[c, y, zh] = hidden.astype(BF16)

    def spread(s, c, yy, zz, k, *peers, which=None):
        ref = gradss[s].at[c, yy, zz] if which is None else gradss[s].at[c, yy, zz, which]
        move(ref, ref, s, c, 3 + k, *peers)

    def spread_y(s, stage, c):
        grads = gradss[s].at[c]
        if stage == 0:
            spread(s, c, y, zh, 0, to_z)
            spread(s, c, y, zh, 1, to_y1, to_y3)
        elif stage == 1:
            wait_for(grads.at[0, 0], recv_sem.at[s, c, 3])
            spread(s, c, y, oz, 1, to_y1, to_y3)
        elif stage == 2:
            wait_for(grads.at[0:2], recv_sem.at[s, c, 4])
            spread(s, c, y3, 0, 2, to_y1)
            spread(s, c, y1, 1, 2, to_y3)
        else:
            wait_for(grads.at[0], recv_sem.at[s, c, 5])
            use(s, c)

    def spread_z(s, stage, c):
        grads = gradss[s].at[c]
        if stage == 0:
            spread(s, c, y, zh, 0, to_y1, to_y3)
            spread(s, c, y, zh, 2, to_z)
        elif stage == 1:
            wait_for(grads.at[0], recv_sem.at[s, c, 3])
            spread(s, c, y3, zh, 1, to_y1, which=low)
            spread(s, c, y1, zh, 1, to_y3, which=high)
            spread(s, c, y1, zh, 2, to_z)
            spread(s, c, y3, zh, 2, to_z)
        elif stage == 2:
            wait_for(grads.at[0, 0], recv_sem.at[s, c, 4])
            spread(s, c, y2, zh, 2, to_z)
        else:
            wait_for(grads.at[0:2], recv_sem.at[s, c, 5])
            use(s, c)

    def to_branch(c):
        def tile(k, _):
            back = lax.dot_general(
                grads0[c, k].reshape(2 * length, 2 * chunk),
                weights[c, :, columns[0]],
                (((1,), (1,)), ((), ())),
                preferred_element_type=F32,
            )
            branch[k] += back.reshape(2, length, depth)
            return 0

        lax.fori_loop(0, 4, tile, 0)

    def leave():
        for r in range(8):
            leaving[r] = branch[r // 2, r % 2].astype(BF16)
        for r in range(8):
            t = (r % 2) * 4 + r // 2
            send(leaving.at[r], landed.at[tp], tail_send, tail_recv, others[t])

    def use(s, c):
        if s == 0:
            to_branch(c)
            pl.when(c == chunks - 1)(leave)
        slot = lax.rem(c, 2)
        staged = stageds[s]

        @pl.when(c >= 2)
        def _():
            wait_for(staged.at[slot], out_sem.at[s, slot])

        m = depth // 3
        scale = 1.0 / math.sqrt(total)

        def tile(k, _):
            at = pl.ds(pl.multiple_of(k * m, m), m)
            right = gradss[s][c].reshape(total, staged.shape[2])
            out = jnp.dot(rows_t[s, at, :], right, preferred_element_type=F32) * scale
            staged[slot, at, :] = out.astype(BF16)
            return 0

        lax.fori_loop(0, 3, tile, 0)
        at = pl.ds(pl.multiple_of(c * chunk, chunk), chunk)
        for k, hbm in enumerate(((gg_hbm, gu_hbm), (gd_hbm,))[s]):
            pltpu.make_async_copy(
                staged.at[slot, :, k * chunk : (k + 1) * chunk], hbm.at[0, :, at], out_sem.at[s, slot]
            ).start()

    def transposes():
        for k in range(2):
            for r in range(8):
                rows_t[k, :, r * length : (r + 1) * length] = rows[k, r // 2, r % 2].T

    def at_step(i, lags, stage, kind, for_y, for_z):
        for name, what in (("z", for_z), ("y", for_y)):
            c = i - lags[name][stage]
            picked = kind(c) if name == "z" else jnp.logical_not(kind(c))

            @pl.when((c >= 0) & (c < chunks) & picked)
            def _():
                what(c)

    def step(i, _):
        @pl.when(i == 1)
        def _():
            head_middle(1)

        @pl.when(i == LAG_SUM[1]["y"][0])
        def _():
            head_end(1)

        for stage in range(3):
            for s in range(2):
                at_step(
                    i, LAG_SUM[s], stage, sums_z,
                    functools.partial(sum_y, s, stage), functools.partial(sum_z, s, stage),
                )
        c = i - LAG_OUT[0]["y"][0]
        for pick, done in ((sums_z(c), final_z), (jnp.logical_not(sums_z(c)), final_y)):

            @pl.when((c >= 0) & (c < chunks) & pick)
            def _():
                finish(c, done)

        for stage in range(4):
            for s in range(2):
                at_step(
                    i, LAG_OUT[s], stage, spreads_z,
                    functools.partial(spread_y, s, stage), functools.partial(spread_z, s, stage),
                )
        pl.when(i == LAG_SUM[1]["y"][0] + 1)(transposes)
        return 0

    lax.fori_loop(0, chunks + LAST, step, 0)

    wait_for(other_cot, cot_sem)
    wait_for(landed, tail_recv)
    summed = landed[0].astype(F32)
    for r in range(1, 8):
        summed = summed + landed[r].astype(F32)
    passed[0] = (other_cot[...].astype(F32) + summed).astype(BF16).T

    def drain(c, _):
        for k in range(2):
            for s in range(2):
                wait_for(arriveds[s].at[c], send_sem.at[k, s, c])
        return 0

    lax.fori_loop(0, chunks, drain, 0)
    for k in range(2):
        wait_for(landed.at[0:7], head_send.at[k])
    wait_for(other_cot, cot_send)
    wait_for(leaving, tail_send)
    for s in range(2):
        for slot in range(2):
            wait_for(stageds[s].at[slot], out_sem.at[s, slot])


def local(normed, cotangent, w_gate, w_up, w_down):
    _, length, depth = normed.shape
    width = w_gate.shape[2]
    chunks = width // CHUNK
    wide = (2 * CHUNK, CHUNK)
    anywhere = pl.BlockSpec(memory_space=pl.ANY)
    dma = pltpu.SemaphoreType.DMA
    flipped = jax.ShapeDtypeStruct((1, depth, length), BF16)
    passed, *grads = pl.pallas_call(
        kernel,
        out_shape=(flipped, *[jax.ShapeDtypeStruct(w_gate.shape, BF16)] * 3),
        in_specs=[anywhere] * 5,
        out_specs=(pl.BlockSpec(memory_space=pltpu.VMEM), anywhere, anywhere, anywhere),
        scratch_shapes=[
            pltpu.VMEM((2, depth, length), BF16),
            pltpu.VMEM((2, 4, 2, length, depth), BF16),
            pltpu.VMEM((2, depth, 8 * length), BF16),
            pltpu.VMEM((chunks, depth, 3 * CHUNK), BF16),
            *[pltpu.VMEM((chunks, 4, 2, length, w), BF16) for w in wide],
            *[pltpu.VMEM((chunks, 7, length, w), BF16) for w in wide],
            *[pltpu.VMEM((chunks, 4, 2, length, w), BF16) for w in wide],
            pltpu.VMEM((4, 2, length, depth), F32),
            *[pltpu.VMEM((2, depth, w), BF16) for w in wide],
            pltpu.VMEM((8, length, depth), BF16),
            pltpu.VMEM((8, length, depth), BF16),
            pltpu.VMEM((length, depth), BF16),
            dma((2,)),
            dma((chunks, 2)),
            dma((2, 2)),
            dma((2, 4)),
            dma((2,)),
            dma((2, chunks, 6)),
            dma((2, 2, chunks)),
            dma(()),
            dma(()),
            dma(()),
            dma(()),
        ],
        compiler_params=pltpu.CompilerParams(
            collective_id=0, has_side_effects=True, vmem_limit_bytes=67_043_328
        ),
        name="geglu_relay",
    )(jnp.swapaxes(normed, 1, 2), jnp.swapaxes(cotangent, 1, 2), w_gate, w_up, w_down)
    return (jnp.swapaxes(passed, 1, 2), *grads)


def solution(mesh):
    in_specs = (
        P("section", "tp", "fsdp"),
        P("section", "tp", "fsdp"),
        P("section", "fsdp", "tp"),
        P("section", "fsdp", "tp"),
        P("section", "fsdp", "tp"),
    )
    out_specs = (
        P("section", "tp", "fsdp"),
        P("section", "fsdp", "tp"),
        P("section", "fsdp", "tp"),
        P("section", "fsdp", "tp"),
    )
    return jax.shard_map(local, mesh=mesh, in_specs=in_specs, out_specs=out_specs, check_vma=False)
```

time: 591 us -> 246 us (0.42)
  waiting for transfers between devices: 455 us -> 0 us
  Pallas kernels: 0 us -> 236 us
  matrix products: 50.6 us -> 0 us
  blocking collectives: 35.3 us -> 0 us
  other arithmetic: 27.1 us -> 0 us
  between operations: 14.1 us -> 0.64 us
  local copies, waits for them, and re-layouts: 2.43 us -> 9.37 us
    reduce_scatter x1 -> x0, waiting for transfers between devices: 293 us -> none  [local(): lax.psum_scatter(jnp.concatenate((gate, up, back), axis=1), 'fsdp', scatt...]
    pallas_call x0 -> x1, Pallas kernels: none -> 236 us  [local(): pl.pallas_call(kernel, out_shape=(flipped, *[jax.ShapeDtypeStruct(w_gate....]
    all_gather x1 -> x0, waiting for transfers between devices: 160 us -> none  [in_one_piece(): lax.all_gather(both, axis, axis=dim, tiled=True)]
    dot_general x8 -> x0, matrix products: 50.6 us -> none  [the longest x3 21.6 us: column_grad(): lax.dot_general(left, right, (((0,), (0,)), ((), ())), preferred_element_...]
    all_to_all x1 -> x0, blocking collectives: 35.3 us -> none  [from_everyone(): return lax.all_to_all(copies, axis, split_axis=0, concat_axis=0, tiled=True)]
    concatenate x3 -> x0, other arithmetic: 22.7 us -> none  [the longest x1 20.3 us: local(): jnp.concatenate((gate, up, back), axis=1)]
    unnamed x15 -> x8, local copies, waits for them, and re-layouts: 0.69 us -> 9.37 us
  transfers between devices with their start and end apart: 4 -> 0, of which waited for: 3 -> 0; matrix products, arithmetic and copies ran while one was open for 4% -> 0% of each run, Pallas kernels for 0% -> 0%
where the time goes in v2:
time: 246 us
  Pallas kernels  236 us (96%)
  local copies, waits for them, and re-layouts  9.37 us (4%)
    pallas_call x1, Pallas kernels, local(): pl.pallas_call(kernel, out_shape=(flipped, *[jax.ShapeDtypeStruct(w_gate....  236 us
    unnamed x8, local copies, waits for them, and re-layouts  9.37 us

profile of v2, /device:TPU:0, one launch (start us, length us, event | category | flops | bytes accessed | tf_op | source)
XLA Modules:
  0.0 245.9 jit_solution(15275422937130662191)
XLA Ops:
  0.6 235.9 %geglu_relay.1 = (bf16[1,576,128]{2,1,0:T(8,128)(2,1)}, bf16[1,576,2304]{2,1,0:T(8,128)(2,1)}, bf16[1,576,2304]{2,1,0:T(8,128)(2,1)}, bf16[1,576,2304]{2,1,0:T(8,128)(2,1)}) custom-call(bf16[1,576,128]{2,1,0:T(8,128)(2,1)} %bitcast.4, bf16[1,576,128]{2,1,0:T(8,128)(2,1)} %bitcast.5, bf16[1,576,2304]{2,1,0:T(8,128)(2,1)} %wg_hbm.1, ...), custom_call_target="tpu_custom_call" | custom-call | tf_op jit(solution)/shard_map/geglu_relay/pallas_call | solution.py:370
  236.5 1.6 copy.13
  238.1 0.0 copy-start.1
  238.1 3.6 %copy.14 = bf16[1,576,2304]{2,1,0:T(8,128)(2,1)} copy(bf16[1,576,2304]{2,1,0:T(8,128)(2,1)} %get-tuple-element.17) | data formatting | bytes 5308416
  241.7 0.0 copy-done.1
  241.7 0.0 copy-start
  241.7 1.5 copy.15
  243.2 1.2 copy-done
  244.4 1.5 copy.16
Async XLA Ops:
  238.1 3.6 %copy-start.1 = (bf16[1,576,2304]{2,1,0:T(8,128)(2,1)S(1)}, bf16[1,576,2304]{2,1,0:T(8,128)(2,1)}, u32[]{:S(2)}) copy-start(bf16[1,576,2304]{2,1,0:T(8,128)(2,1)} %get-tuple-element.18) | copy-start | bytes 7962628
  241.7 2.7 %copy-start = (bf16[1,576,2304]{2,1,0:T(8,128)(2,1)S(1)}, bf16[1,576,2304]{2,1,0:T(8,128)(2,1)}, u32[]{:S(2)}) copy-start(bf16[1,576,2304]{2,1,0:T(8,128)(2,1)} %get-tuple-element.19) | copy-start | bytes 7962628

commit v3 on v2

--- a/solution.py
+++ b/solution.py
@@ -10,9 +10,43 @@
 
 MESH = pl.DeviceIdType.MESH
 CHUNK = 256
-LAG_SUM = ({"y": (0, 2, 3), "z": (0, 2, 3)}, {"y": (3, 4, 6), "z": (3, 4, 6)})
-LAG_OUT = ({"y": (7, 8, 9, 10), "z": (7, 8, 9, 10)}, {"y": (13, 14, 15, 16), "z": (13, 14, 15, 17)})
-LAST = 17
+SUMS_Z = (2, 4, 5, 6)
+SPREADS_Z = (0, 1, 7)
+LAGS = {
+    (0, 0): (0, 0),
+    (0, 1): (20, 4),
+    (0, 2): (27, 22),
+    (0, 3): (46, 46),
+    (0, 4): (81, 79),
+    (0, 5): (84, 84),
+    (0, 6): (90, 89),
+    (1, 0): (6, 6),
+    (1, 1): (28, 12),
+    (1, 2): (40, 27),
+    (1, 3): (84, 87),
+    (1, 4): (90, 93),
+    (1, 5): (96, 99),
+    (1, 6): (105, 105),
+}
+ORDER = (
+    (1, 1),
+    (1, 6),
+    (1, 5),
+    (1, 0),
+    (1, 2),
+    (1, 3),
+    (1, 4),
+    (0, 0),
+    (0, 3),
+    (0, 1),
+    (0, 2),
+    (0, 6),
+    (0, 4),
+    (0, 5),
+)
+HEAD_AT = 4
+BACK_AT = 6
+LAST = 105
 F32 = jnp.float32
 BF16 = jnp.bfloat16
 
@@ -27,22 +61,18 @@
     return act * up, back * up * slope, back * act
 
 
-def sums_z(c):
-    return (c > 0) & (lax.rem(c, 2) == 0)
-
-
-def spreads_z(c):
-    return lax.rem(c, 2) == 1
+def among(c, members):
+    return functools.reduce(jnp.logical_or, [c == m for m in members])
 
 
 def kernel(
     n_hbm, c_hbm, wg_hbm, wu_hbm, wd_hbm,
-    passed, gg_hbm, gu_hbm, gd_hbm,
+    passed, grad_gate, grad_up, grad_down,
     own, rows, rows_t, weights, part0, part1, arrived0, arrived1, grads0, grads1, branch,
-    staged0, staged1, leaving, landed, other_cot,
-    load_sem, weight_sem, out_sem, head_sem, head_send, recv_sem, send_sem, tail_recv, tail_send, cot_sem, cot_send,
+    landed, other_cot,
+    load_sem, weight_sem, head_sem, head_send, recv_sem, send_sem, tail_recv, tail_send, cot_sem, cot_send,
 ):
-    parts, arriveds, gradss, stageds = (part0, part1), (arrived0, arrived1), (grads0, grads1), (staged0, staged1)
+    parts, arriveds, gradss = (part0, part1), (arrived0, arrived1), (grads0, grads1)
     chunks = weights.shape[0]
     chunk = weights.shape[2] // 3
     depth = rows.shape[4]
@@ -119,10 +149,10 @@
 
     pl.semaphore_wait(barrier, len(peers))
     head_start(0)
+    head_middle(0)
     head_start(1)
     send(rows.at[1, x, zl], other_cot, cot_send, cot_sem, {"section": 1 - section})
     branch[...] = jnp.zeros_like(branch)
-    head_middle(0)
     head_end(0)
 
     def forward(s, c):
@@ -255,83 +285,67 @@
         lax.fori_loop(0, 4, tile, 0)
 
     def leave():
+        for k in range(2):
+            wait_for(landed.at[0:7], head_send.at[k])
         for r in range(8):
-            leaving[r] = branch[r // 2, r % 2].astype(BF16)
+            rows[0, r // 2, r % 2] = branch[r // 2, r % 2].astype(BF16)
         for r in range(8):
             t = (r % 2) * 4 + r // 2
-            send(leaving.at[r], landed.at[tp], tail_send, tail_recv, others[t])
+            send(rows.at[0, r // 2, r % 2], landed.at[tp], tail_send, tail_recv, others[t])
 
     def use(s, c):
         if s == 0:
             to_branch(c)
             pl.when(c == chunks - 1)(leave)
-        slot = lax.rem(c, 2)
-        staged = stageds[s]
-
-        @pl.when(c >= 2)
-        def _():
-            wait_for(staged.at[slot], out_sem.at[s, slot])
-
         m = depth // 3
         scale = 1.0 / math.sqrt(total)
 
         def tile(k, _):
             at = pl.ds(pl.multiple_of(k * m, m), m)
-            right = gradss[s][c].reshape(total, staged.shape[2])
-            out = jnp.dot(rows_t[s, at, :], right, preferred_element_type=F32) * scale
-            staged[slot, at, :] = out.astype(BF16)
+            right = gradss[s][c].reshape(total, gradss[s].shape[4])
+            out = (jnp.dot(rows_t[s, at, :], right, preferred_element_type=F32) * scale).astype(BF16)
+            for q, ref in enumerate(((grad_gate, grad_up), (grad_down,))[s]):
+                ref[0, at, pl.ds(pl.multiple_of(c * chunk, chunk), chunk)] = out[:, q * chunk : (q + 1) * chunk]
             return 0
 
         lax.fori_loop(0, 3, tile, 0)
-        at = pl.ds(pl.multiple_of(c * chunk, chunk), chunk)
-        for k, hbm in enumerate(((gg_hbm, gu_hbm), (gd_hbm,))[s]):
-            pltpu.make_async_copy(
-                staged.at[slot, :, k * chunk : (k + 1) * chunk], hbm.at[0, :, at], out_sem.at[s, slot]
-            ).start()
 
     def transposes():
         for k in range(2):
             for r in range(8):
                 rows_t[k, :, r * length : (r + 1) * length] = rows[k, r // 2, r % 2].T
 
-    def at_step(i, lags, stage, kind, for_y, for_z):
-        for name, what in (("z", for_z), ("y", for_y)):
-            c = i - lags[name][stage]
-            picked = kind(c) if name == "z" else jnp.logical_not(kind(c))
+    def at_step(i, lags, members, for_y, for_z):
+        for lag, what, z in zip(lags, (for_z, for_y), (True, False)):
+            c = i - lag
+            picked = among(c, members) if z else jnp.logical_not(among(c, members))
 
             @pl.when((c >= 0) & (c < chunks) & picked)
             def _():
                 what(c)
 
     def step(i, _):
-        @pl.when(i == 1)
-        def _():
-            head_middle(1)
-
-        @pl.when(i == LAG_SUM[1]["y"][0])
+        pl.when(i == HEAD_AT)(functools.partial(head_middle, 1))
+
+        @pl.when(i == BACK_AT)
         def _():
             head_end(1)
 
-        for stage in range(3):
-            for s in range(2):
+        for s, stage in ORDER:
+            if stage < 3:
+                bind = functools.partial
+                at_step(i, LAGS[s, stage], SUMS_Z, bind(sum_y, s, stage), bind(sum_z, s, stage))
+            else:
+                if (s, stage) == (0, 3):
+                    at_step(
+                        i, LAGS[s, stage], SUMS_Z,
+                        functools.partial(finish, done=final_y), functools.partial(finish, done=final_z),
+                    )
                 at_step(
-                    i, LAG_SUM[s], stage, sums_z,
-                    functools.partial(sum_y, s, stage), functools.partial(sum_z, s, stage),
+                    i, LAGS[s, stage], SPREADS_Z,
+                    functools.partial(spread_y, s, stage - 3), functools.partial(spread_z, s, stage - 3),
                 )
-        c = i - LAG_OUT[0]["y"][0]
-        for pick, done in ((sums_z(c), final_z), (jnp.logical_not(sums_z(c)), final_y)):
-
-            @pl.when((c >= 0) & (c < chunks) & pick)
-            def _():
-                finish(c, done)
-
-        for stage in range(4):
-            for s in range(2):
-                at_step(
-                    i, LAG_OUT[s], stage, spreads_z,
-                    functools.partial(spread_y, s, stage), functools.partial(spread_z, s, stage),
-                )
-        pl.when(i == LAG_SUM[1]["y"][0] + 1)(transposes)
+        pl.when(i == BACK_AT + 1)(transposes)
         return 0
 
     lax.fori_loop(0, chunks + LAST, step, 0)
@@ -350,13 +364,8 @@
         return 0
 
     lax.fori_loop(0, chunks, drain, 0)
-    for k in range(2):
-        wait_for(landed.at[0:7], head_send.at[k])
     wait_for(other_cot, cot_send)
-    wait_for(leaving, tail_send)
-    for s in range(2):
-        for slot in range(2):
-            wait_for(stageds[s].at[slot], out_sem.at[s, slot])
+    wait_for(rows.at[0], tail_send)
 
 
 def local(normed, cotangent, w_gate, w_up, w_down):
@@ -366,12 +375,11 @@
     wide = (2 * CHUNK, CHUNK)
     anywhere = pl.BlockSpec(memory_space=pl.ANY)
     dma = pltpu.SemaphoreType.DMA
-    flipped = jax.ShapeDtypeStruct((1, depth, length), BF16)
     passed, *grads = pl.pallas_call(
         kernel,
-        out_shape=(flipped, *[jax.ShapeDtypeStruct(w_gate.shape, BF16)] * 3),
+        out_shape=(pltpu.VMEM((1, depth, length), BF16), *[pltpu.VMEM(w_gate.shape, BF16)] * 3),
         in_specs=[anywhere] * 5,
-        out_specs=(pl.BlockSpec(memory_space=pltpu.VMEM), anywhere, anywhere, anywhere),
+        out_specs=(pl.BlockSpec(memory_space=pltpu.VMEM),) * 4,
         scratch_shapes=[
             pltpu.VMEM((2, depth, length), BF16),
             pltpu.VMEM((2, 4, 2, length, depth), BF16),
@@ -381,13 +389,10 @@
             *[pltpu.VMEM((chunks, 7, length, w), BF16) for w in wide],
             *[pltpu.VMEM((chunks, 4, 2, length, w), BF16) for w in wide],
             pltpu.VMEM((4, 2, length, depth), F32),
-            *[pltpu.VMEM((2, depth, w), BF16) for w in wide],
-            pltpu.VMEM((8, length, depth), BF16),
             pltpu.VMEM((8, length, depth), BF16),
             pltpu.VMEM((length, depth), BF16),
             dma((2,)),
             dma((chunks, 2)),
-            dma((2, 2)),
             dma((2, 4)),
             dma((2,)),
             dma((2, chunks, 6)),
@@ -398,7 +403,7 @@
             dma(()),
         ],
         compiler_params=pltpu.CompilerParams(
-            collective_id=0, has_side_effects=True, vmem_limit_bytes=67_043_328
+            collective_id=0, has_side_effects=True, vmem_limit_bytes=58_800_000
         ),
         name="geglu_relay",
     )(jnp.swapaxes(normed, 1, 2), jnp.swapaxes(cotangent, 1, 2), w_gate, w_up, w_down)

time: 246 us -> 223 us (0.907)
  Pallas kernels: 236 us -> 216 us
  local copies, waits for them, and re-layouts: 9.37 us -> 5.17 us
    pallas_call x1, Pallas kernels: 236 us -> 216 us  [local(): pl.pallas_call(kernel, out_shape=(pltpu.VMEM((1, depth, length), BF16), *...]
    unnamed x8 -> x4, local copies, waits for them, and re-layouts: 9.37 us -> 5.17 us
where the time goes in v3:
time: 223 us; the launch traced here: 222 us
  Pallas kernels  216 us (97%)
  local copies, waits for them, and re-layouts  5.17 us (2%)
    pallas_call x1, Pallas kernels, local(): pl.pallas_call(kernel, out_shape=(pltpu.VMEM((1, depth, length), BF16), *...  216 us
    unnamed x4, local copies, waits for them, and re-layouts  5.17 us

profile of v3, /device:TPU:0, one launch (start us, length us, event | category | flops | bytes accessed | tf_op | source)
XLA Modules:
  0.0 221.8 jit_solution(16302150225054587580)
XLA Ops:
  0.6 215.9 %geglu_relay.1 = (bf16[1,576,128]{2,1,0:T(8,128)(2,1)S(1)}, bf16[1,576,2304]{2,1,0:T(8,128)(2,1)S(1)}, bf16[1,576,2304]{2,1,0:T(8,128)(2,1)S(1)}, bf16[1,576,2304]{2,1,0:T(8,128)(2,1)S(1)}) custom-call(bf16[1,576,128]{2,1,0:T(8,128)(2,1)} %bitcast.4, bf16[1,576,128]{2,1,0:T(8,128)(2,1)} %bitcast.5, bf16[1,576,2304]{2,1,0:T(8,128)(2,1)} %wg_hbm.1, ...), custom_call_target="tpu_custom_call" | custom-call | tf_op jit(solution)/shard_map/geglu_relay/pallas_call | solution.py:378
  216.6 0.7 copy.13
  217.3 1.5 copy.14
  218.8 1.5 copy.15
  220.3 1.5 copy.16

commit v4 on v3

--- a/solution.py
+++ b/solution.py
@@ -105,6 +105,45 @@
     for peer in peers:
         pl.semaphore_signal(barrier, inc=1, device_id=peer, device_id_type=MESH)
 
+    def ready(k):
+        loads[k].wait()
+        rows[k, x, zl] = own[k].T
+
+    ready(0)
+
+    def send(src, dst, sender, recv, peer):
+        pltpu.make_async_remote_copy(
+            src_ref=src, dst_ref=dst, send_sem=sender, recv_sem=recv, device_id=peer, device_id_type=MESH
+        ).start()
+
+    def wait_for(ref, sem):
+        pltpu.make_async_copy(ref, ref, sem).wait()
+
+    def head(k, xx, ll, which, sem, *peers):
+        ref = rows.at[k, xx, ll, which]
+        for peer in peers:
+            send(ref, ref, head_send.at[k], head_sem.at[k, sem], peer)
+
+    def head_start(k):
+        head(k, x, zl, high, 2, to_x1, to_x3, to_x2)
+        head(k, x, zl, low, 0, to_l)
+        head(k, x, zl, high, 3, to_l)
+        head(k, x, zl, low, 1, to_x1, to_x3, to_x2)
+
+    def head_middle(k):
+        wait_for(rows.at[k, 0, 0, low], head_sem.at[k, 0])
+        head(k, x, ol, low, 1, to_x1, to_x3, to_x2)
+        wait_for(rows.at[k, 0:3, 0, low], head_sem.at[k, 2])
+        for xx in (x1, x3, x2):
+            head(k, xx, zl, high, 3, to_l)
+
+    def head_end(k):
+        wait_for(rows.at[k, 0:3, 0], head_sem.at[k, 1])
+        wait_for(rows.at[k, 0:2, 0], head_sem.at[k, 3])
+
+    pl.semaphore_wait(barrier, len(peers))
+    head_start(0)
+
     for t in range(chunks):
         for k, hbm in enumerate((wg_hbm, wu_hbm, wd_hbm)):
             pltpu.make_async_copy(
@@ -113,42 +152,7 @@
                 weight_sem.at[t, k // 2],
             ).start()
 
-    for k, load in enumerate(loads):
-        load.wait()
-        rows[k, x, zl] = own[k].T
-
-    def send(src, dst, sender, recv, peer):
-        pltpu.make_async_remote_copy(
-            src_ref=src, dst_ref=dst, send_sem=sender, recv_sem=recv, device_id=peer, device_id_type=MESH
-        ).start()
-
-    def wait_for(ref, sem):
-        pltpu.make_async_copy(ref, ref, sem).wait()
-
-    def head(k, xx, ll, which, sem, *peers):
-        ref = rows.at[k, xx, ll, which]
-        for peer in peers:
-            send(ref, ref, head_send.at[k], head_sem.at[k, sem], peer)
-
-    def head_start(k):
-        head(k, x, zl, high, 2, to_x1, to_x3, to_x2)
-        head(k, x, zl, low, 0, to_l)
-        head(k, x, zl, high, 3, to_l)
-        head(k, x, zl, low, 1, to_x1, to_x3, to_x2)
-
-    def head_middle(k):
-        wait_for(rows.at[k, 0, 0, low], head_sem.at[k, 0])
-        head(k, x, ol, low, 1, to_x1, to_x3, to_x2)
-        wait_for(rows.at[k, 0:3, 0, low], head_sem.at[k, 2])
-        for xx in (x1, x3, x2):
-            head(k, xx, zl, high, 3, to_l)
-
-    def head_end(k):
-        wait_for(rows.at[k, 0:3, 0], head_sem.at[k, 1])
-        wait_for(rows.at[k, 0:2, 0], head_sem.at[k, 3])
-
-    pl.semaphore_wait(barrier, len(peers))
-    head_start(0)
+    ready(1)
     head_middle(0)
     head_start(1)
     send(rows.at[1, x, zl], other_cot, cot_send, cot_sem, {"section": 1 - section})

time: 223 us -> 223 us (level)
  no operation moved by 1% of the time
where the time goes in v4:
time: 223 us; the launch traced here: 222 us
  Pallas kernels  216 us (97%)
  local copies, waits for them, and re-layouts  5.17 us (2%)
    pallas_call x1, Pallas kernels, local(): pl.pallas_call(kernel, out_shape=(pltpu.VMEM((1, depth, length), BF16), *...  216 us
    unnamed x4, local copies, waits for them, and re-layouts  5.17 us

profile of v4, /device:TPU:0, one launch (start us, length us, event | category | flops | bytes accessed | tf_op | source)
XLA Modules:
  0.0 221.8 jit_solution(9610246303965934772)
XLA Ops:
  0.6 215.9 %geglu_relay.1 = (bf16[1,576,128]{2,1,0:T(8,128)(2,1)S(1)}, bf16[1,576,2304]{2,1,0:T(8,128)(2,1)S(1)}, bf16[1,576,2304]{2,1,0:T(8,128)(2,1)S(1)}, bf16[1,576,2304]{2,1,0:T(8,128)(2,1)S(1)}) custom-call(bf16[1,576,128]{2,1,0:T(8,128)(2,1)} %bitcast.4, bf16[1,576,128]{2,1,0:T(8,128)(2,1)} %bitcast.5, bf16[1,576,2304]{2,1,0:T(8,128)(2,1)} %wg_hbm.1, ...), custom_call_target="tpu_custom_call" | custom-call | tf_op jit(solution)/shard_map/geglu_relay/pallas_call | solution.py:382
  216.6 0.7 copy.13
  217.2 1.5 copy.14
  218.8 1.5 copy.15
  220.3 1.5 copy.16

commit v5 on v4

--- a/solution.py
+++ b/solution.py
@@ -79,7 +79,7 @@
     length = rows.shape[3]
     half = length // 2
     total = 8 * length
-    low, high = pl.ds(0, half), pl.ds(half, half)
+    low, high, whole = pl.ds(0, half), pl.ds(half, half), pl.ds(0, length)
     columns = (pl.ds(0, 2 * chunk), pl.ds(2 * chunk, chunk))
     section = lax.axis_index("section")
     tp = lax.axis_index("tp")
@@ -137,6 +137,17 @@
         for xx in (x1, x3, x2):
             head(k, xx, zl, high, 3, to_l)
 
+    def cot_start():
+        head(1, x, zl, whole, 0, to_l)
+        head(1, x, zl, whole, 1, to_x1, to_x3, to_x2)
+
+    def cot_middle():
+        wait_for(rows.at[1, 0, 0], head_sem.at[1, 0])
+        head(1, x, ol, whole, 1, to_x1, to_x3, to_x2)
+
+    def cot_end():
+        wait_for(rows.at[1, 0:3], head_sem.at[1, 1])
+
     def head_end(k):
         wait_for(rows.at[k, 0:3, 0], head_sem.at[k, 1])
         wait_for(rows.at[k, 0:2, 0], head_sem.at[k, 3])
@@ -154,7 +165,7 @@
 
     ready(1)
     head_middle(0)
-    head_start(1)
+    cot_start()
     send(rows.at[1, x, zl], other_cot, cot_send, cot_sem, {"section": 1 - section})
     branch[...] = jnp.zeros_like(branch)
     head_end(0)
@@ -329,11 +340,9 @@
                 what(c)
 
     def step(i, _):
-        pl.when(i == HEAD_AT)(functools.partial(head_middle, 1))
-
-        @pl.when(i == BACK_AT)
-        def _():
-            head_end(1)
+        pl.when(i == HEAD_AT)(cot_middle)
+
+        pl.when(i == BACK_AT)(cot_end)
 
         for s, stage in ORDER:
             if stage < 3:

time: 223 us -> 218 us (0.978)
  Pallas kernels: 216 us -> 212 us
    pallas_call x1, Pallas kernels: 216 us -> 212 us  [local(): pl.pallas_call(kernel, out_shape=(pltpu.VMEM((1, depth, length), BF16), *...]
where the time goes in v5:
time: 218 us
  Pallas kernels  212 us (97%)
  local copies, waits for them, and re-layouts  5.17 us (2%)
    pallas_call x1, Pallas kernels, local(): pl.pallas_call(kernel, out_shape=(pltpu.VMEM((1, depth, length), BF16), *...  212 us
    unnamed x4, local copies, waits for them, and re-layouts  5.17 us

profile of v5, /device:TPU:0, one launch (start us, length us, event | category | flops | bytes accessed | tf_op | source)
XLA Modules:
  0.0 218.0 jit_solution(14646069976675984337)
XLA Ops:
  0.6 212.2 %geglu_relay.1 = (bf16[1,576,128]{2,1,0:T(8,128)(2,1)S(1)}, bf16[1,576,2304]{2,1,0:T(8,128)(2,1)S(1)}, bf16[1,576,2304]{2,1,0:T(8,128)(2,1)S(1)}, bf16[1,576,2304]{2,1,0:T(8,128)(2,1)S(1)}) custom-call(bf16[1,576,128]{2,1,0:T(8,128)(2,1)} %bitcast.4, bf16[1,576,128]{2,1,0:T(8,128)(2,1)} %bitcast.5, bf16[1,576,2304]{2,1,0:T(8,128)(2,1)} %wg_hbm.1, ...), custom_call_target="tpu_custom_call" | custom-call | tf_op jit(solution)/shard_map/geglu_relay/pallas_call | solution.py:391
  212.9 0.7 copy.13
  213.5 1.5 copy.14
  215.0 1.5 copy.15
  216.5 1.5 copy.16

commit v6 on v5

--- a/solution.py
+++ b/solution.py
@@ -44,7 +44,7 @@
     (0, 4),
     (0, 5),
 )
-HEAD_AT = 4
+HEAD_AT = 1
 BACK_AT = 6
 LAST = 105
 F32 = jnp.float32

time: 218 us -> 219 us (level)
  no operation moved by 1% of the time
where the time goes in v6:
time: 219 us
  Pallas kernels  213 us (97%)
  local copies, waits for them, and re-layouts  5.17 us (2%)
    pallas_call x1, Pallas kernels, local(): pl.pallas_call(kernel, out_shape=(pltpu.VMEM((1, depth, length), BF16), *...  213 us
    unnamed x4, local copies, waits for them, and re-layouts  5.17 us

profile of v6, /device:TPU:0, one launch (start us, length us, event | category | flops | bytes accessed | tf_op | source)
XLA Modules:
  0.0 218.6 jit_solution(1953831680766432592)
XLA Ops:
  0.6 212.8 %geglu_relay.1 = (bf16[1,576,128]{2,1,0:T(8,128)(2,1)S(1)}, bf16[1,576,2304]{2,1,0:T(8,128)(2,1)S(1)}, bf16[1,576,2304]{2,1,0:T(8,128)(2,1)S(1)}, bf16[1,576,2304]{2,1,0:T(8,128)(2,1)S(1)}) custom-call(bf16[1,576,128]{2,1,0:T(8,128)(2,1)} %bitcast.4, bf16[1,576,128]{2,1,0:T(8,128)(2,1)} %bitcast.5, bf16[1,576,2304]{2,1,0:T(8,128)(2,1)} %wg_hbm.1, ...), custom_call_target="tpu_custom_call" | custom-call | tf_op jit(solution)/shard_map/geglu_relay/pallas_call | solution.py:391
  213.4 0.7 copy.13
  214.1 1.5 copy.14
  215.6 1.5 copy.15
  217.1 1.5 copy.16
